TPU v7x, 16 devices: a whole 2x2x2 slice. The times are simulated.
16 devices in a mesh: col: 2 (over z), row: 8 (over y, x, core).
Axes of the slice: x: 2, y: 2, z: 2, core: 2. Of those that a mesh axis runs over, the one named last changes fastest.
Arguments:
- adjacency: bfloat16 [24576, 24576], P('row', 'col')
- pers_vec: float32 [24576, 64], P(('row', 'col'))
- restart_wt: float32 [16, 64], replicated
Outputs:
- output 1: float32 [24576, 64], P(('col', 'row'))
- output 2: float32 [24576, 64], P(('row', 'col'))
All inputs are finite; a program needn't handle non-finite values.
Results may differ from a plain program's by a relative error of at most 0.001.
Values are sent between devices in bfloat16 or wider.
A program may use at most 1 GiB of HBM per device.

v0:
```python
import functools

import jax
import jax.numpy as jnp
from jax import lax
from jax.experimental import pallas as pl
from jax.experimental.pallas import tpu as pltpu
from jax.sharding import PartitionSpec as P

F32, BF16 = jnp.float32, jnp.bfloat16
MESH = pl.DeviceIdType.MESH
SLOTS = 6


def prod_cols(lhs, rhs):
    return lax.dot_general(lhs, rhs, (((1,), (0,)), ((), ())), preferred_element_type=F32)


def prod_rows(lhs, rhs, zero):
    cols = []
    size_m, size_n = min(256, rhs.shape[0]), min(256, rhs.shape[1])
    for r in range(0, rhs.shape[0], size_m):
        val = None
        for c in range(0, rhs.shape[1], size_n):
            tile = rhs[r:r + size_m, c:c + size_n]
            if (c // size_n) % 3 == 2:
                part = lax.dot_general(lhs[:, c:c + size_n], tile, (((1,), (1,)), ((), ())), preferred_element_type=F32)
            else:
                tile = tile.T
                tile = tile + jnp.tile(zero, (tile.shape[0] // zero.shape[0], tile.shape[1] // zero.shape[1]))
                part = prod_cols(lhs[:, c:c + size_n], tile)
            val = part if val is None else val + part
        cols.append(val)
    return jnp.concatenate(cols, axis=1)


def lane_tile(v, width):
    return jnp.concatenate([v] * (width // 128), axis=1)


def row_to_lanes(row, dim):
    return jnp.broadcast_to(row, (128, 128)).T[:dim]


def square_sums(parts):
    total = None
    for part in parts:
        for t in range(part.shape[1] // 128):
            v = part[:, t * 128:(t + 1) * 128]
            total = v * v if total is None else total + v * v
    full = jnp.concatenate([total, jnp.zeros((128 - total.shape[0], 128), F32)], axis=0)
    row = jnp.sum(full.T, axis=0, keepdims=True)
    return jnp.broadcast_to(row, (8, 128))


def kernel(n_total, v_ref, b_ref, a_hbm, auth_out, hub_out,
           res, stm, vt, bt, hb, ab, acc, own_sum, oth_sum, rd, s1x, s1y, s2x, s2y, zr, none_ref, sq_send, sq1, sq2,
           res_sem, stm_sem, dd_s, dd_r, x1_s, x1_r, y1_s, y1_r, x2_s, x2_r, y2_s, y2_r,
           ag_s, ag_r, z_s, z_r, h_s, h_r, q1_s, q1_r, q2_s, q2_r):
    sweeps, dim = b_ref.shape
    rows, width = stm.shape[1], stm.shape[2]
    groups, span = oth_sum.shape[0], oth_sum.shape[2]
    j, i = lax.axis_index("col"), lax.axis_index("row")
    core, x, y = i % 2, (i // 2) % 2, i // 4
    partner = {"row": i + 1 - 2 * core, "col": j}
    xnb = {"row": i + 2 - 4 * x, "col": j}
    ynb = {"row": i + 4 - 8 * y, "col": j}
    znb = {"row": i, "col": 1 - j}
    base_o, base_x = 4 * y + 2 * x, 4 * y + 2 * (1 - x)
    base_y, base_d = 4 * (1 - y) + 2 * x, 4 * (1 - y) + 2 * (1 - x)
    mine, other = core, 1 - core
    ord1 = [base_d + other, base_d + mine, base_x + other, base_x + mine,
            base_y + other, base_y + mine, base_o + mine, base_o + other]
    ord2 = [base_o + mine, base_o + other, base_x + mine, base_y + mine,
            base_x + other, base_y + other, base_d + other, base_d + mine]

    def rcopy(src, dst, s, r, dev):
        return pltpu.make_async_remote_copy(src, dst, s, r, device_id=dev, device_id_type=MESH)

    def a_block(which, chunk, half):
        return a_hbm.at[pl.ds(pl.multiple_of(which * rows, rows), rows),
                        pl.ds(pl.multiple_of((chunk * 2 + half) * width, width), width)]

    def load(chunk, half, slot, own):
        return pltpu.make_async_copy(a_block(j if own else 1 - j, chunk, half), stm.at[slot], stm_sem.at[slot])

    def load_res(q, half, own):
        return pltpu.make_async_copy(a_block(j if own else 1 - j, ord1[q], half), res.at[ord1[q], half],
                                     res_sem.at[2 * q + half])

    def block_wait(ci, order, far):
        slots = [(2 * ci + half) % SLOTS for half in range(2)]
        if ci >= 2:
            for half in range(2):
                load(order[ci], half, slots[half], ci in far).wait()
        return slots

    def block_next(ci, order, after, far, half=None):
        for h in range(2) if half is None else (half,):
            slot = (2 * ci + h) % SLOTS
            if ci <= 4:
                load(order[ci + 3], h, slot, ci + 3 in far).start()
            elif ci == 5:
                load(after[2], h, slot, False).start()

    def copies_h():
        return [rcopy(hb.at[0, part], hb.at[1, part], h_s.at[part], h_r.at[part], znb) for part in range(2)]

    def send_h(val):
        for part in range(2):
            hb[0, part] = val[:, part * width:(part + 1) * width].astype(BF16)
        for c in copies_h():
            c.start()

    def cols_of(which, blocks):
        return prod_cols(jnp.concatenate([hb[which, 0], hb[which, 1]], axis=1), blocks)

    def own_near():
        def pair(t, c):
            for base in (base_x, base_y):
                for half in range(2):
                    acc[base + t, half] = cols_of(0, res[base + t, half])
            return c
        lax.fori_loop(0, 2, pair, 0)

    def all_sum(row8, buf, send, recv):
        sq_send[...] = row8
        buf[0] = row8
        copies = []
        for d in range(15, 0, -1):
            dz, dy, dx, dc = d // 8, (d // 4) % 2, (d // 2) % 2, d % 2
            dev = {"row": 4 * ((y + dy) % 2) + 2 * ((x + dx) % 2) + (core + dc) % 2, "col": (j + dz) % 2}
            copies.append(rcopy(sq_send, buf.at[d], send.at[d], recv.at[d], dev))
            copies[-1].start()
        for c in copies:
            c.wait_recv()
        vals = [buf[d] for d in range(16)]
        while len(vals) > 1:
            vals = [vals[q] + vals[q + 1] for q in range(0, len(vals), 2)]
        scale = lax.rsqrt(vals[0] / n_total)
        cols = row_to_lanes(scale[:1], dim)
        for c in copies:
            c.wait_send()
        return cols

    none_ref[...] = jnp.zeros(none_ref.shape, BF16)
    for u in range(4):
        load(ord1[u // 2], u % 2, u, True).start()
    for q in (2, 3, 4, 5, 0, 1):
        for half in range(2):
            load_res(q, half, q >= 2).start()
    for half in range(2):
        load(ord1[2], half, 4 + half, False).start()
    for q in (6, 7):
        for half in range(2):
            load_res(q, half, True).start()
    barrier = pltpu.get_barrier_semaphore()
    for d in range(1, 16):
        dz, dy, dx, dc = d // 8, (d // 4) % 2, (d // 2) % 2, d % 2
        dev = {"row": 4 * ((y + dy) % 2) + 2 * ((x + dx) % 2) + (core + dc) % 2, "col": (j + dz) % 2}
        pl.semaphore_signal(barrier, inc=1, device_id=dev, device_id_type=MESH)
    pad = jnp.zeros((128, 128 - dim), F32)
    for t in range(rows // 128):
        tile = jnp.concatenate([v_ref[t * 128:(t + 1) * 128, :], pad], axis=1)
        vt[:, t * 128:(t + 1) * 128] = tile.T[:dim]
    pl.semaphore_wait(barrier, 15)
    send_h(vt[...])
    for k in range(sweeps):
        bt[k] = row_to_lanes(jnp.concatenate([b_ref[k:k + 1, :], pad[:1]], axis=1), dim)

    for q in range(2):
        for half in range(2):
            load(ord1[q], half, 2 * q + half, True).wait()
    far1, far2 = (0, 1), (6, 7)

    def own_far():
        for q in range(2):
            for half in range(2):
                acc[ord1[q], half] = cols_of(0, stm[2 * q + half])
        for q in range(2):
            block_next(q, ord1, ord2, far1)

    own_far()
    for q in range(2, 6):
        for half in range(2):
            load_res(q, half, True).wait()
    own_near()
    for q in (0, 1, 6, 7):
        for half in range(2):
            load_res(q, half, q >= 6).wait()

    def sweep(k, carry):
        with jax.named_scope("hwait"):
            h_cps = copies_h()
            h_cps[0].wait_recv()
        h_cps[1].wait_recv()
        d_mine, x_mine, y_mine, o_mine = ord1[1], ord1[3], ord1[5], ord1[6]
        gives = [ord1[0], ord1[2], ord1[4], ord1[7]]
        keeps = [d_mine, x_mine, y_mine, o_mine]
        dd = [rcopy(acc.at[gives[t]], rd.at[t], dd_s.at[t], dd_r.at[t], partner) for t in range(4)]
        x1 = [rcopy(acc.at[d_mine, 0], s1x.at[0], x1_s.at[0], x1_r.at[0], xnb),
              rcopy(acc.at[x_mine, 0], s1x.at[1], x1_s.at[1], x1_r.at[1], xnb)]
        y1 = [rcopy(acc.at[d_mine, 1], s1y.at[0], y1_s.at[0], y1_r.at[0], ynb),
              rcopy(acc.at[y_mine, 1], s1y.at[1], y1_s.at[1], y1_r.at[1], ynb)]
        x2 = rcopy(acc.at[x_mine, 1], s2x, x2_s, x2_r, xnb)
        y2 = rcopy(acc.at[y_mine, 0], s2y, y2_s, y2_r, ynb)

        def far_rows(ci):
            for half in range(2):
                acc[ord1[ci], half] += cols_of(1, res[ord1[ci], half])

        def other_rows(ci):
            chunk = ord1[ci]
            slots = block_wait(ci, ord1, far1)
            for half in range(2):
                val = cols_of(1, stm[slots[half]])
                if ci >= 6:
                    acc[chunk, half] = cols_of(0, res[chunk, half]) + val
                else:
                    acc[chunk, half] += val
            block_next(ci, ord1, ord2, far1)

        def combine(t):
            dd[t].wait_recv()
            acc[keeps[t]] += rd[t]

        with jax.named_scope("p1a"):
            far_rows(0)
            dd[0].start()
            far_rows(1)
            other_rows(2)
            dd[1].start()
        with jax.named_scope("comb0"):
            combine(0)
            x1[0].start()
            y1[0].start()
        with jax.named_scope("p1b"):
            other_rows(3)
            other_rows(4)
            dd[2].start()
        with jax.named_scope("comb1"):
            combine(1)
            x1[1].start()
        with jax.named_scope("p1c"):
            other_rows(5)
        with jax.named_scope("comb2"):
            combine(2)
            y1[1].start()
        with jax.named_scope("p1d"):
            other_rows(6)
            other_rows(7)
            dd[3].start()
        with jax.named_scope("rs2"):
            x1[0].wait_recv()
            acc[y_mine, 0] += s1x[0]
            y2.start()
            y1[0].wait_recv()
            acc[x_mine, 1] += s1y[0]
            x2.start()
        with jax.named_scope("rs3"):
            combine(3)
            x1[1].wait_recv()
            y1[1].wait_recv()
            p0 = acc[o_mine, 0] + s1x[1]
            p1 = acc[o_mine, 1] + s1y[1]
            acc[o_mine, 0] = p0
            acc[o_mine, 1] = p1
        with jax.named_scope("rs4"):
            y2.wait_recv()
            x2.wait_recv()
            p0 = acc[o_mine, 0] + s2y[...]
            p1 = acc[o_mine, 1] + s2x[...]
            auth_out[0] = p0
            auth_out[1] = p1
        with jax.named_scope("ar1"):
            scale = all_sum(square_sums([p0, p1]), sq1, q1_s, q1_r)
        with jax.named_scope("norm1"):
            wide = lane_tile(scale, width)
            for half in range(2):
                val = auth_out[half] * wide
                auth_out[half] = val
                ab[i, half] = val.astype(BF16)
            for c in dd + x1 + y1 + [x2, y2, *h_cps]:
                c.wait_send()

        px, py, pd = ord1[3], ord1[5], ord1[1]
        to_p = rcopy(ab.at[i], ab.at[i], ag_s.at[0], ag_r.at[0], partner)
        to_x = [rcopy(ab.at[i, h], ab.at[i, h], ag_s.at[1 + h], ag_r.at[1 + h], xnb) for h in range(2)]
        to_y = [rcopy(ab.at[i, h], ab.at[i, h], ag_s.at[3 + h], ag_r.at[3 + h], ynb) for h in range(2)]
        rel_y = rcopy(ab.at[px, 0], ab.at[px, 0], ag_s.at[5], ag_r.at[5], ynb)
        rel_x = rcopy(ab.at[py, 1], ab.at[py, 1], ag_s.at[6], ag_r.at[6], xnb)
        fw_x = rcopy(ab.at[px], ab.at[px], ag_s.at[7], ag_r.at[7], partner)
        fw_y = rcopy(ab.at[py], ab.at[py], ag_s.at[8], ag_r.at[8], partner)
        fw_d = rcopy(ab.at[pd], ab.at[pd], ag_s.at[9], ag_r.at[9], partner)
        to_p.start()
        to_x[0].start()
        to_y[1].start()
        to_x[1].start()
        to_y[0].start()

        zero = none_ref[...]

        def rows_of(chunk, half, block):
            return prod_rows(ab[chunk, half], block, zero)

        def resident(chunk):
            return rows_of(chunk, 0, res[chunk, 0]) + rows_of(chunk, 1, res[chunk, 1])

        def add_other(val, first=False):
            for g in range(groups):
                part = val[:, g * span:(g + 1) * span]
                if first:
                    oth_sum[g] = part
                else:
                    oth_sum[g] += part

        def streamed(ci, first=False):
            chunk = ord2[ci]
            slots = block_wait(ci, ord2, far2)
            add_other(rows_of(chunk, 0, stm[slots[0]]) + rows_of(chunk, 1, stm[slots[1]]), first)
            block_next(ci, ord2, ord1, far2)

        with jax.named_scope("p2a"):
            streamed(0, first=True)
        with jax.named_scope("pwait"):
            to_p.wait_recv()
        with jax.named_scope("p2b"):
            streamed(1)
            own_sum[...] = resident(ord2[0]) + resident(ord2[1])
        with jax.named_scope("xwait"):
            to_x[0].wait_recv()
            rel_y.start()
            to_y[1].wait_recv()
            rel_x.start()
        with jax.named_scope("p2c"):
            slots = block_wait(2, ord2, far2) + block_wait(3, ord2, far2)
            add_other(rows_of(ord2[2], 0, stm[slots[0]]) + rows_of(ord2[3], 1, stm[slots[3]]))
            block_next(2, ord2, ord1, far2, 0)
            block_next(3, ord2, ord1, far2, 1)
        with jax.named_scope("xwait2"):
            to_x[1].wait_recv()
            fw_x.start()
            to_y[0].wait_recv()
            fw_y.start()
        with jax.named_scope("p2d"):
            add_other(rows_of(ord2[2], 1, stm[slots[1]]) + rows_of(ord2[3], 0, stm[slots[2]]))
            block_next(2, ord2, ord1, far2, 1)
            block_next(3, ord2, ord1, far2, 0)
        with jax.named_scope("fxwait"):
            fw_x.wait_recv()
        with jax.named_scope("p2e"):
            streamed(4)
        with jax.named_scope("dwait"):
            rel_y.wait_recv()
            rel_x.wait_recv()
            fw_d.start()
            fw_y.wait_recv()
        with jax.named_scope("p2f"):
            streamed(5)
        with jax.named_scope("fdwait"):
            fw_d.wait_recv()
        with jax.named_scope("p2g"):
            z_cps = [rcopy(oth_sum.at[g], zr.at[g], z_s.at[g], z_r.at[g], znb) for g in range(groups)]
            for g in range(groups):
                val = oth_sum[g]
                for q in (6, 7):
                    for half in range(2):
                        val += rows_of(ord2[q], half, res[ord2[q], half, g * span:(g + 1) * span, :])
                oth_sum[g] = val
                z_cps[g].start()

        with jax.named_scope("p2rest"):
            def pair(t, c):
                own_sum[...] += resident(base_x + t) + resident(base_y + t)
                return c
            lax.fori_loop(0, 2, pair, 0)
            slots = block_wait(6, ord2, far2) + block_wait(7, ord2, far2)
            for q in range(4):
                own_sum[...] += rows_of(ord2[6 + q // 2], q % 2, stm[slots[q]])
        with jax.named_scope("zwait"):
            for g in range(groups):
                z_cps[g].wait_recv()
        with jax.named_scope("ar2"):
            val = own_sum[...] + jnp.concatenate([zr[g] for g in range(groups)], axis=1)
            own_sum[...] = val
            scale = all_sum(square_sums([val]), sq2, q2_s, q2_r)
        with jax.named_scope("upd"):
            wt = bt[k]
            hv = lane_tile(1.0 - wt, rows) * (own_sum[...] * lane_tile(scale, rows)) + lane_tile(wt, rows) * vt[...]
            hub_out[...] = hv
            for c in [to_p, *to_x, *to_y, rel_y, rel_x, fw_x, fw_y, fw_d, *z_cps]:
                c.wait_send()

        with jax.named_scope("own"):
            @pl.when(k < sweeps - 1)
            def _():
                send_h(hub_out[...])
                own_far()
                own_near()
        return carry

    lax.fori_loop(0, sweeps, sweep, 0)
    for half in range(2):
        load(ord1[2], half, 4 + half, False).wait()


def solution(mesh):
    def device_fn(adj_tile, pers_piece, restart_wt):
        sweeps, dim = restart_wt.shape
        chunk = pers_piece.shape[0]
        width = chunk // 2
        n_total = float(chunk * mesh.size)
        groups = 3 if chunk % 384 == 0 else 2
        vmem = pl.BlockSpec(memory_space=pltpu.VMEM)
        dma = pltpu.SemaphoreType.DMA
        auth, hub = pl.pallas_call(
            functools.partial(kernel, n_total),
            out_shape=(jax.ShapeDtypeStruct((2, dim, width), F32), jax.ShapeDtypeStruct((dim, chunk), F32)),
            in_specs=[vmem, vmem, pl.BlockSpec(memory_space=pl.ANY)],
            out_specs=(vmem, vmem),
            scratch_shapes=[
                pltpu.VMEM((8, 2, chunk, width), BF16),
                pltpu.VMEM((SLOTS, chunk, width), BF16),
                pltpu.VMEM((dim, chunk), F32),
                pltpu.VMEM((sweeps, dim, 128), F32),
                pltpu.VMEM((2, 2, dim, width), BF16),
                pltpu.VMEM((8, 2, dim, width), BF16),
                pltpu.VMEM((8, 2, dim, width), F32),
                pltpu.VMEM((dim, chunk), F32),
                pltpu.VMEM((groups, dim, chunk // groups), F32),
                pltpu.VMEM((4, 2, dim, width), F32),
                pltpu.VMEM((2, dim, width), F32),
                pltpu.VMEM((2, dim, width), F32),
                pltpu.VMEM((dim, width), F32),
                pltpu.VMEM((dim, width), F32),
                pltpu.VMEM((groups, dim, chunk // groups), F32),
                pltpu.VMEM((16, 128), BF16),
                pltpu.VMEM((8, 128), F32),
                pltpu.VMEM((16, 8, 128), F32),
                pltpu.VMEM((16, 8, 128), F32),
                dma((16,)), dma((SLOTS,)), dma((4,)), dma((4,)), dma((2,)), dma((2,)), dma((2,)), dma((2,)),
                dma, dma, dma, dma, dma((10,)), dma((10,)), dma((groups,)), dma((groups,)), dma((2,)), dma((2,)),
                dma((16,)), dma((16,)), dma((16,)), dma((16,)),
            ],
            compiler_params=pltpu.CompilerParams(vmem_limit_bytes=67043328, has_side_effects=True, collective_id=0),
        )(pers_piece, restart_wt, adj_tile)
        return auth.transpose(0, 2, 1).reshape(chunk, dim), hub.T

    return jax.shard_map(
        device_fn, mesh=mesh,
        in_specs=(P("row", "col"), P(("row", "col"), None), P(None, None)),
        out_specs=(P(("col", "row"), None), P(("row", "col"), None)), check_vma=False)
```

profile of v0, /device:TPU:0, one launch (start us, length us, event | category | flops | bytes accessed | tf_op | source)
XLA Modules:
  0.0 866.1 jit_solution(9265256138310517669)
XLA Ops:
  0.6 2.2 copy.6.v_ref
  2.8 859.8 %shard_map.50 = (f32[2,64,768]{2,1,0:T(8,128)}, f32[64,1536]{1,0:T(8,128)}) custom-call(f32[1536,64]{1,0:T(8,128)} %copy.6.v_ref, f32[16,64]{1,0:T(8,128)} %b_ref.1, bf16[3072,12288]{1,0:T(8,128)(2,1)} %a_hbm.1), custom_call_target="tpu_custom_call" | custom-call | tf_op jit(solution)/shard_map/pallas_call | solution.py:416
  862.6 1.8 copy.8
  864.3 1.8 copy.10
where the time goes:
time: 866 us
  Pallas kernels  860 us (99%)
    pallas_call x1, Pallas kernels, device_fn(): pl.pallas_call(functools.partial(kernel, n_total), out_shape=(jax.ShapeDt...  860 us

commit v1 on v0

--- a/solution.py
+++ b/solution.py
@@ -410,7 +410,7 @@
         chunk = pers_piece.shape[0]
         width = chunk // 2
         n_total = float(chunk * mesh.size)
-        groups = 3 if chunk % 384 == 0 else 2
+        groups = 6 if chunk % 768 == 0 else 2
         vmem = pl.BlockSpec(memory_space=pltpu.VMEM)
         dma = pltpu.SemaphoreType.DMA
         auth, hub = pl.pallas_call(

time: 866 us -> 871 us (level)
  no operation moved by 1% of the time
where the time goes in v1:
time: 871 us; the launch traced here: 870 us
  Pallas kernels  864 us (99%)
    pallas_call x1, Pallas kernels, device_fn(): pl.pallas_call(functools.partial(kernel, n_total), out_shape=(jax.ShapeDt...  864 us

profile of v1, /device:TPU:0, one launch (start us, length us, event | category | flops | bytes accessed | tf_op | source)
XLA Modules:
  0.0 870.4 jit_solution(13066022979300813050)
XLA Ops:
  0.6 2.2 copy.6.v_ref
  2.8 864.0 %shard_map.50 = (f32[2,64,768]{2,1,0:T(8,128)}, f32[64,1536]{1,0:T(8,128)}) custom-call(f32[1536,64]{1,0:T(8,128)} %copy.6.v_ref, f32[16,64]{1,0:T(8,128)} %b_ref.1, bf16[3072,12288]{1,0:T(8,128)(2,1)} %a_hbm.1), custom_call_target="tpu_custom_call" | custom-call | tf_op jit(solution)/shard_map/pallas_call | solution.py:416
  866.8 1.8 copy.8
  868.6 1.8 copy.10
